TPU v7x, 32 devices: a whole 2x2x4 slice. The times are simulated.
32 devices in a mesh: cuts: 8 (over z, x), mode: 4 (over y, core).
Axes of the slice: x: 2, y: 2, z: 4, core: 2. Of those that a mesh axis runs over, the one named last changes fastest.
Arguments:
- sliced_state: bfloat16 [8, 16, 4, 128, 2, 128], P(None, 'cuts', None, 'mode'), may hold values from -0.75 to 0.75
- gate_blocks: bfloat16 [32, 2, 128, 128], P('cuts'), may hold values from -0.375 to 0.375
- gate_slot: int32 [32], replicated, may hold values from 0 to 31, each once
- samples: int32 [8, 4096], replicated, may hold values from 0 to 65535
Outputs:
- amplitudes: float32 [32, 128, 2, 128], P('cuts', 'mode')
- sample_probs: float32 [8, 4096], replicated
- xeb_score: float32 [8], replicated
Inputs may be any that keep to these rules, and one draw needn't show every extreme that they name: `gate_slot`: a permutation: every gate block has its own row of gate_blocks. `samples`: flat index s * 128 * 128 + p * 128 + q.
All inputs are finite; a program needn't handle non-finite values.
Results may differ from a plain program's by a relative error of at most 0.022.
Values may be sent and summed in bfloat16 or wider, within the bound.
A program may use at most 64 MiB of HBM per device.

v0:
```python
import jax
import jax.numpy as jnp
from jax import lax
from jax.sharding import PartitionSpec as P


def from_root(array, axis, root):
    mine = lax.axis_index(axis) == root
    return lax.psum(jnp.where(mine, array, jnp.zeros_like(array)), axis)


def apply_gates(tensor, blocks):
    real_part = blocks[:, 0]
    imag_part = blocks[:, 1]
    stacked = jnp.concatenate(
        [
            jnp.concatenate([real_part, imag_part], axis=2),
            jnp.concatenate([-imag_part, real_part], axis=2),
        ],
        axis=1,
    )
    layout = tensor.shape
    flattened = tensor.reshape(layout[0], -1, 2 * layout[-1])
    product = jnp.einsum("crk,ckn->crn", flattened, stacked, preferred_element_type=jnp.float32)
    return product.astype(jnp.bfloat16).reshape(layout)


def select_rows(table, wanted):
    count = table.shape[0]
    onehot = (wanted[:, None] == jnp.arange(count, dtype=jnp.int32)[None, :]).astype(table.dtype)
    picked = jnp.dot(onehot, table.reshape(count, -1), preferred_element_type=jnp.float32)
    return picked.astype(table.dtype).reshape((wanted.shape[0],) + table.shape[1:])


def on_device(sliced_state, gate_blocks, gate_slot, samples):
    circuits = sliced_state.shape[0]
    spectator = sliced_state.shape[2]
    width = sliced_state.shape[5]
    held_count = gate_blocks.shape[0]
    layer_count = gate_slot.shape[0] // (2 * circuits)
    circuit_ids = jnp.arange(circuits, dtype=jnp.int32)
    tensor = lax.all_to_all(sliced_state, "mode", split_axis=0, concat_axis=3, tiled=True)
    local_count = tensor.shape[0]
    local_ids = lax.axis_index("mode") * local_count + jnp.arange(local_count, dtype=jnp.int32)

    def fetch_one(position):
        held_block = select_rows(gate_blocks, jnp.reshape(position % held_count, (1,)))[0]
        return from_root(held_block, "cuts", position // held_count)

    def fetch_gates(layer_index, gate_kind):
        fetched = []
        for circuit in range(local_count):
            fetched.append(
                fetch_one(
                    gate_slot[(local_ids[circuit] * layer_count + layer_index) * 2 + gate_kind]
                )
            )
        return jnp.stack(fetched, axis=0)

    for layer_index in range(layer_count):
        tensor = apply_gates(tensor, fetch_gates(layer_index, 0))
        tensor = jnp.swapaxes(tensor, 3, 5)
        tensor = apply_gates(tensor, fetch_gates(layer_index, 1))
        tensor = jnp.swapaxes(tensor, 3, 5)
    summed = jnp.sum(tensor.astype(jnp.float32), axis=1)
    summed = lax.all_to_all(
        summed.astype(jnp.bfloat16), "mode", split_axis=2, concat_axis=0, tiled=True
    ).astype(summed.dtype)
    local_rows = summed.shape[2]
    summed = summed.reshape(circuits * spectator, local_rows, 2, width)
    amplitudes = lax.psum_scatter(
        summed.astype(jnp.bfloat16), "cuts", scatter_dimension=0, tiled=True
    ).astype(jnp.float32)
    row_count = amplitudes.shape[0]
    first_row = lax.axis_index("cuts") * row_count
    first_col = lax.axis_index("mode") * local_rows
    magnitude = amplitudes[:, :, 0, :] ** 2 + amplitudes[:, :, 1, :] ** 2
    row_sums = jnp.sum(magnitude, axis=(1, 2))
    owner_circuit = (first_row + jnp.arange(row_count, dtype=jnp.int32)) // spectator
    norm_part = jnp.sum(
        jnp.where(owner_circuit[None, :] == circuit_ids[:, None], row_sums[None, :], 0.0), axis=1
    )
    plane_size = width * width
    spec_index = samples // plane_size
    row_index = samples // width % width
    col_index = samples % width
    local_row = circuit_ids[:, None] * spectator + spec_index - first_row
    local_col = row_index - first_col
    is_owned = (
        (local_row >= 0) & (local_row < row_count) & (local_col >= 0) & (local_col < local_rows)
    )
    cell_index = jnp.where(is_owned, local_row * local_rows + local_col, -1)
    cell_count = row_count * local_rows
    cell_onehot = (
        cell_index[:, :, None] == jnp.arange(cell_count, dtype=jnp.int32)[None, None, :]
    ).astype(jnp.float32)
    picked_rows = jnp.einsum(
        "csr,rw->csw",
        cell_onehot,
        magnitude.reshape(cell_count, width),
        precision=lax.Precision.HIGHEST,
    )
    col_match = col_index[:, :, None] == jnp.arange(width, dtype=jnp.int32)[None, None, :]
    sample_mass = jnp.sum(jnp.where(col_match, picked_rows, 0.0), axis=2)
    dimension_scale = float(spectator * plane_size)
    norm_total = lax.psum(norm_part, ("cuts", "mode"))
    sample_probs = lax.psum(sample_mass * dimension_scale / norm_total[:, None], ("cuts", "mode"))
    xeb_score = jnp.mean(sample_probs, axis=1)
    return (amplitudes, sample_probs, xeb_score)


def solution(mesh):
    in_specs = (P(None, "cuts", None, "mode", None, None), P("cuts", None, None, None), P(), P())
    out_specs = (P("cuts", "mode", None, None), P(), P())
    return jax.shard_map(
        on_device, mesh=mesh, in_specs=in_specs, out_specs=out_specs, check_vma=False
    )
```

profile of v0, /device:TPU:0, one launch (start us, length us, event | category | flops | bytes accessed | tf_op | source)
XLA Modules:
  0.0 402.5 jit_solution(14701239896464762398)
XLA Ops:
  7.2 0.0 all-reduce.6.cloned.1.call-start
  7.2 0.6 fusion.74
  10.4 1.6 fusion.73
  32.4 1.2 copy.56
  33.6 0.3 fusion.39
  33.9 0.7 copy.39
  34.7 0.3 fusion.40
  35.0 0.7 copy.40
  35.8 0.3 fusion.41
  36.1 0.3 fusion.42
  36.4 0.3 fusion.43
  36.7 0.3 fusion.44
  37.1 0.3 fusion.45
  37.4 0.3 fusion.46
  37.7 0.6 convert_select_fusion.5
  38.3 0.6 convert_select_fusion.4
  39.0 0.6 convert_select_fusion.3
  39.6 0.6 convert_select_fusion.2
  40.2 0.6 convert_select_fusion.1
  40.8 0.6 convert_select_fusion
  41.5 0.0 all-reduce.6.cloned.1.call-update
  41.5 4.3 %all-to-all-start = ((bf16[8,2,4,32,2,128]{5,4,3,2,1,0:T(2,128)(2,1)}), bf16[8,2,4,32,2,128]{5,4,3,2,1,0:T(2,128)(2,1)S(1)}, u32[]{:S(2)}, u32[]{:S(2)}) async-start(bf16[8,2,4,32,2,128]{5,4,3,2,1,0:T(2,128)(2,1)} %param.4), calls=%async_computation | async-start | bytes 2097152 | tf_op jit(solution)/shard_map/all_to_all | solution.py:42
  45.8 72.8 %all-reduce.6.cloned.1.call-done = (bf16[1,2,128,128]{2,3,0,1:T(8,128)(2,1)}, bf16[1,2,128,128]{2,3,0,1:T(8,128)(2,1)}, bf16[1,2,128,128]{3,2,0,1:T(8,128)(2,1)}...) async-done(((bf16[1,2,128,128]{2,3,0,1:T(8,128)(2,1)}, ...) | async-done | bytes 524304 | tf_op jit(solution)/shard_map/psum | solution.py:9
  118.6 0.9 constant_dynamic-update-slice_fusion.1
  119.5 0.9 constant_dynamic-update-slice_fusion
  120.4 0.8 constant_dynamic-update-slice_fusion.3
  121.2 0.8 constant_dynamic-update-slice_fusion.5
  122.1 0.9 constant_dynamic-update-slice_fusion.2
  123.1 1.2 copy.55
  124.4 0.7 reshape.305
  125.1 0.5 fusion.2
  125.5 0.8 reshape.306
  126.3 1.1 copy.42
  127.4 0.7 reshape.307
  128.1 0.4 convolution_convert_fusion.2
  128.6 0.3 reshape.308
  128.9 1.2 copy.43
  130.1 0.7 reshape.309
  130.8 0.4 convolution_convert_fusion.1
  131.2 0.3 reshape.310
  131.5 1.2 copy.44
  132.8 0.7 reshape.311
  133.5 0.4 convolution_convert_fusion
  133.9 0.3 reshape.312
  134.2 2.4 reduce_sum.50
  136.7 0.7 copy.45
  137.4 11.4 %all_to_all.33 = bf16[2,4,128,2,128]{4,3,1,0,2:T(2,128)(2,1)S(1)} all-to-all(bf16[2,4,128,2,128]{4,3,1,0,2:T(2,128)(2,1)S(1)} %copy.45), channel_id=1, replica_groups=mesh['cuts'=8,'mode'=4] {'mode'}, dimensions={2} | all-to-all | bytes 1048576 | tf_op jit(solution)/shard_map/all_to_all | solution.py:66
  148.8 0.1 copy.46
  148.9 0.8 copy.47
  149.8 0.0 reduce-scatter.2.cloned.1.call-update
  149.8 0.0 all-reduce.4.cloned.1.call-start
  149.9 61.7 %reduce-scatter.2.cloned.1.call-done = bf16[4,32,2,128]{3,1,2,0:T(8,128)(2,1)} async-done(((bf16[32,32,2,128]{3,1,2,0:T(8,128)(2,1)}), bf16[4,32,2,128]{3,1,2,0:T(8,128)(2,1)}) %reduce-scatter.2.cloned.1.call-update) | async-done | bytes 65552 | tf_op jit(solution)/shard_map/reduce_scatter | solution.py:71
  211.5 0.8 convert_element_type.77
  212.4 0.1 fusion.71
  212.5 0.1 select_reduce_fusion.1
  212.6 0.3 add_select_fusion.4
  212.9 40.1 %psum.78 = f32[8]{0:T(128)S(1)} all-reduce(f32[8]{0:T(128)S(1)} %select_reduce_fusion.1), channel_id=1, replica_groups=mesh['cuts'=8,'mode'=4] {'cuts','mode'}, use_global_device_ids=true, to_apply=%region_13.14 | all-reduce | flops 8 | bytes 64 | tf_op jit(solution)/shard_map/psum | solution.py:106
  252.9 15.4 %select_reduce_fusion = f32[8,4096]{1,0:T(8,128)S(1)} fusion(s32[8,4096]{1,0:T(8,128)S(1)} %get-tuple-element.23, f32[128,128,1]{1,0,2:T(8,128)S(1)} %bitcast.154, s32[8,4096]{1,0:T(8,128)S(1)} %get-tuple-element.22), kind=kOutput, calls=%fused_computation | convolution fusion | flops 6459195392 | bytes 458752 | tf_op jit(solution)/shard_map/csr,rw->csw/dot_general | solution.py:97
  268.4 0.7 multiply_divide_fusion
  269.2 0.7 copy.49
  269.9 123.0 %all-reduce.4.cloned.1.call-done = f32[8,4096]{1,0:T(8,128)} async-done(((f32[8,4096]{1,0:T(8,128)}), f32[8,4096]{1,0:T(8,128)}) %all-reduce.4.cloned.1.call-update) | async-done | bytes 131088 | tf_op jit(solution)/shard_map/psum | solution.py:107
  392.8 1.1 reduce_sum.55
  393.9 0.5 broadcast_multiply_fusion
  394.4 1.6 copy.70
  (26 shorter events, 0.2 us)
Async XLA Ops:
  7.2 111.4 %all-reduce.6.cloned.1.call-start = ((), (), s32[]{:S(2)}) async-start(), calls=%async_computation.5 | async-start | bytes 1048576 | tf_op jit(solution)/shard_map/psum | solution.py:9
  41.5 81.6 %all-to-all-start = ((bf16[8,2,4,32,2,128]{5,4,3,2,1,0:T(2,128)(2,1)}), bf16[8,2,4,32,2,128]{5,4,3,2,1,0:T(2,128)(2,1)S(1)}, u32[]{:S(2)}, u32[]{:S(2)}) async-start(bf16[8,2,4,32,2,128]{5,4,3,2,1,0:T(2,128)(2,1)} %param.4), calls=%async_computation | async-start | bytes 2097152 | tf_op jit(solution)/shard_map/all_to_all | solution.py:42
  45.8 165.8 %reduce-scatter.2.cloned.1.call-start = ((), (), s32[]{:S(2)}) async-start(), calls=%async_computation.3 | async-start | bytes 589824 | tf_op jit(solution)/shard_map/reduce_scatter | solution.py:71
  118.6 4.4 %copy-start.3 = (bf16[1,2,128,128]{3,2,0,1:T(8,128)(2,1)S(1)}, bf16[1,2,128,128]{3,2,0,1:T(8,128)(2,1)}, u32[]{:S(2)}) copy-start(bf16[1,2,128,128]{3,2,0,1:T(8,128)(2,1)} %get-tuple-element.18) | copy-start | bytes 196612
  118.6 4.4 %copy-start.2 = (bf16[1,2,128,128]{3,2,0,1:T(8,128)(2,1)S(1)}, bf16[1,2,128,128]{3,2,0,1:T(8,128)(2,1)}, u32[]{:S(2)}) copy-start(bf16[1,2,128,128]{3,2,0,1:T(8,128)(2,1)} %get-tuple-element.19) | copy-start | bytes 196612
  148.9 63.7 %copy-start.1 = (s32[8,4096]{1,0:T(8,128)S(1)}, s32[8,4096]{1,0:T(8,128)}, u32[]{:S(2)}) copy-start(s32[8,4096]{1,0:T(8,128)} %param.7) | copy-start | bytes 393220
  149.8 243.0 %all-reduce.4.cloned.1.call-start = ((), (), s32[]{:S(2)}) async-start(), calls=%async_computation.4 | async-start | bytes 262144 | tf_op jit(solution)/shard_map/psum | solution.py:107
  252.9 16.2 %copy-start = (bf16[4,32,2,128]{3,1,2,0:T(8,128)(2,1)S(1)}, bf16[4,32,2,128]{3,1,2,0:T(8,128)(2,1)}, u32[]{:S(2)}) copy-start(bf16[4,32,2,128]{3,1,2,0:T(8,128)(2,1)} %reduce-scatter.2.cloned.1.call-done) | copy-start | bytes 196612
Sparse Core Ops, SparseCore 0:
  41.6 76.9 all-reduce.5
  149.9 61.5 reduce-scatter.1
  269.3 123.5 all-reduce.3
where the time goes:
time: 403 us; the launch traced here: 402 us
  waiting for transfers between devices  257 us (64%)
  blocking collectives  51.4 us (13%)
  between operations  37.4 us (9%)
  local copies, waits for them, and re-layouts  22.5 us (6%)
  matrix products  19.5 us (5%)
  other arithmetic  9.91 us (2%)
  starting transfers between devices  4.36 us (1%)
    psum x1, waiting for transfers between devices, on_device(): lax.psum(sample_mass * dimension_scale / norm_total[:, None], ('cuts', 'm...  123 us
    psum x1, waiting for transfers between devices, from_root(): return lax.psum(jnp.where(mine, array, jnp.zeros_like(array)), axis)  72.8 us
    reduce_scatter x1, waiting for transfers between devices, on_device(): lax.psum_scatter(summed.astype(jnp.bfloat16), 'cuts', scatter_dimension=0...  61.7 us
    psum x1, blocking collectives, on_device(): norm_total = lax.psum(norm_part, ('cuts', 'mode'))  40.1 us
    dot_general x1, matrix products, on_device(): jnp.einsum('csr,rw->csw', cell_onehot, magnitude.reshape(cell_count, widt...  15.4 us
    all_to_all x1, blocking collectives, on_device(): lax.all_to_all(summed.astype(jnp.bfloat16), 'mode', split_axis=2, concat_...  11.4 us
  transfers between devices with their start and end apart: 4, of which 3 were waited for; matrix products, arithmetic and copies ran while one was open for 1% of the time, Pallas kernels for 0%

commit v1 on v0

--- a/solution.py
+++ b/solution.py
@@ -104,7 +104,9 @@
     sample_mass = jnp.sum(jnp.where(col_match, picked_rows, 0.0), axis=2)
     dimension_scale = float(spectator * plane_size)
     norm_total = lax.psum(norm_part, ("cuts", "mode"))
-    sample_probs = lax.psum(sample_mass * dimension_scale / norm_total[:, None], ("cuts", "mode"))
+    sample_probs = sample_mass * dimension_scale / norm_total[:, None]
+    for mesh_axis in ("mode", "cuts"):
+        sample_probs = lax.psum(sample_probs, mesh_axis)
     xeb_score = jnp.mean(sample_probs, axis=1)
     return (amplitudes, sample_probs, xeb_score)
 

time: 403 us -> 384 us (0.953)
  waiting for transfers between devices: 257 us -> 238 us
    psum x1 -> x2, waiting for transfers between devices: 123 us -> 104 us  [on_device(): sample_probs = lax.psum(sample_probs, mesh_axis)]
  transfers between devices with their start and end apart: 4 -> 5, of which waited for: 3 -> 4; matrix products, arithmetic and copies ran while one was open for 1% -> 1% of each run, Pallas kernels for 0% -> 0%
where the time goes in v1:
time: 384 us; the launch traced here: 383 us
  waiting for transfers between devices  238 us (62%)
  blocking collectives  51.4 us (13%)
  between operations  37.4 us (10%)
  local copies, waits for them, and re-layouts  22.5 us (6%)
  matrix products  19.5 us (5%)
  other arithmetic  9.91 us (3%)
  starting transfers between devices  4.4 us (1%)
    psum x2, waiting for transfers between devices, on_device(): sample_probs = lax.psum(sample_probs, mesh_axis)  104 us
    psum x1, waiting for transfers between devices, from_root(): return lax.psum(jnp.where(mine, array, jnp.zeros_like(array)), axis)  72.8 us
    reduce_scatter x1, waiting for transfers between devices, on_device(): lax.psum_scatter(summed.astype(jnp.bfloat16), 'cuts', scatter_dimension=0...  61.7 us
    psum x1, blocking collectives, on_device(): norm_total = lax.psum(norm_part, ('cuts', 'mode'))  40.1 us
    dot_general x1, matrix products, on_device(): jnp.einsum('csr,rw->csw', cell_onehot, magnitude.reshape(cell_count, widt...  15.4 us
    all_to_all x1, blocking collectives, on_device(): lax.all_to_all(summed.astype(jnp.bfloat16), 'mode', split_axis=2, concat_...  11.4 us
  transfers between devices with their start and end apart: 5, of which 4 were waited for; matrix products, arithmetic and copies ran while one was open for 1% of the time, Pallas kernels for 0%

profile of v1, /device:TPU:0, one launch (start us, length us, event | category | flops | bytes accessed | tf_op | source)
XLA Modules:
  0.0 383.4 jit_solution(8037686019942547713)
XLA Ops:
  7.2 0.0 all-reduce.9.cloned.1.call-start
  7.2 0.6 fusion.74
  10.4 1.6 fusion.73
  32.4 1.2 copy.56
  33.6 0.3 fusion.39
  33.9 0.7 copy.39
  34.7 0.3 fusion.40
  35.0 0.7 copy.40
  35.8 0.3 fusion.41
  36.1 0.3 fusion.42
  36.4 0.3 fusion.43
  36.7 0.3 fusion.44
  37.1 0.3 fusion.45
  37.4 0.3 fusion.46
  37.7 0.6 convert_select_fusion.5
  38.3 0.6 convert_select_fusion.4
  39.0 0.6 convert_select_fusion.3
  39.6 0.6 convert_select_fusion.2
  40.2 0.6 convert_select_fusion.1
  40.8 0.6 convert_select_fusion
  41.5 4.3 %all-to-all-start = ((bf16[8,2,4,32,2,128]{5,4,3,2,1,0:T(2,128)(2,1)}), bf16[8,2,4,32,2,128]{5,4,3,2,1,0:T(2,128)(2,1)S(1)}, u32[]{:S(2)}, u32[]{:S(2)}) async-start(bf16[8,2,4,32,2,128]{5,4,3,2,1,0:T(2,128)(2,1)} %param.4), calls=%async_computation | async-start | bytes 2097152 | tf_op jit(solution)/shard_map/all_to_all | solution.py:42
  45.8 72.8 %all-reduce.9.cloned.1.call-done = (bf16[1,2,128,128]{2,3,0,1:T(8,128)(2,1)}, bf16[1,2,128,128]{2,3,0,1:T(8,128)(2,1)}, bf16[1,2,128,128]{3,2,0,1:T(8,128)(2,1)}...) async-done(((bf16[1,2,128,128]{2,3,0,1:T(8,128)(2,1)}, ...) | async-done | bytes 524304 | tf_op jit(solution)/shard_map/psum | solution.py:9
  118.6 0.9 constant_dynamic-update-slice_fusion.1
  119.5 0.9 constant_dynamic-update-slice_fusion
  120.4 0.8 constant_dynamic-update-slice_fusion.3
  121.2 0.8 constant_dynamic-update-slice_fusion.5
  122.1 0.9 constant_dynamic-update-slice_fusion.2
  123.1 1.2 copy.55
  124.4 0.7 reshape.305
  125.1 0.5 fusion.2
  125.5 0.8 reshape.306
  126.3 1.1 copy.42
  127.4 0.7 reshape.307
  128.1 0.4 convolution_convert_fusion.2
  128.6 0.3 reshape.308
  128.9 1.2 copy.43
  130.1 0.7 reshape.309
  130.8 0.4 convolution_convert_fusion.1
  131.2 0.3 reshape.310
  131.5 1.2 copy.44
  132.8 0.7 reshape.311
  133.5 0.4 convolution_convert_fusion
  133.9 0.3 reshape.312
  134.2 2.4 reduce_sum.50
  136.7 0.7 copy.45
  137.4 11.4 %all_to_all.33 = bf16[2,4,128,2,128]{4,3,1,0,2:T(2,128)(2,1)S(1)} all-to-all(bf16[2,4,128,2,128]{4,3,1,0,2:T(2,128)(2,1)S(1)} %copy.45), channel_id=1, replica_groups=mesh['cuts'=8,'mode'=4] {'mode'}, dimensions={2} | all-to-all | bytes 1048576 | tf_op jit(solution)/shard_map/all_to_all | solution.py:66
  148.8 0.1 copy.46
  148.9 0.8 copy.47
  149.8 0.0 all-reduce.5.cloned.1.call-start
  149.9 61.7 %reduce-scatter.2.cloned.1.call-done = bf16[4,32,2,128]{3,1,2,0:T(8,128)(2,1)} async-done(((bf16[32,32,2,128]{3,1,2,0:T(8,128)(2,1)}), bf16[4,32,2,128]{3,1,2,0:T(8,128)(2,1)}) %reduce-scatter.2.cloned.1.call-update) | async-done | bytes 65552 | tf_op jit(solution)/shard_map/reduce_scatter | solution.py:71
  211.5 0.8 convert_element_type.77
  212.4 0.1 fusion.71
  212.5 0.1 select_reduce_fusion.1
  212.6 0.3 add_select_fusion.4
  212.9 40.1 %psum.85 = f32[8]{0:T(128)S(1)} all-reduce(f32[8]{0:T(128)S(1)} %select_reduce_fusion.1), channel_id=1, replica_groups=mesh['cuts'=8,'mode'=4] {'cuts','mode'}, use_global_device_ids=true, to_apply=%region_13.14 | all-reduce | flops 8 | bytes 64 | tf_op jit(solution)/shard_map/psum | solution.py:106
  253.0 15.4 %select_reduce_fusion = f32[8,4096]{1,0:T(8,128)S(1)} fusion(s32[8,4096]{1,0:T(8,128)S(1)} %get-tuple-element.23, f32[128,128,1]{1,0,2:T(8,128)S(1)} %bitcast.154, s32[8,4096]{1,0:T(8,128)S(1)} %get-tuple-element.22), kind=kOutput, calls=%fused_computation | convolution fusion | flops 6459195392 | bytes 458752 | tf_op jit(solution)/shard_map/csr,rw->csw/dot_general | solution.py:97
  268.4 0.7 multiply_divide_fusion
  269.2 0.0 all-reduce.7.cloned.1.call-start
  269.2 30.8 %all-reduce.5.cloned.1.call-done = f32[8,4096]{1,0:T(8,128)} async-done(((f32[8,4096]{1,0:T(8,128)}), f32[8,4096]{1,0:T(8,128)}) %all-reduce.5.cloned.1.call-update) | async-done | bytes 131088 | tf_op jit(solution)/shard_map/psum | solution.py:109
  300.1 0.7 copy.49
  300.8 73.0 %all-reduce.7.cloned.1.call-done = f32[8,4096]{1,0:T(8,128)} async-done(((f32[8,4096]{1,0:T(8,128)}), f32[8,4096]{1,0:T(8,128)}) %all-reduce.7.cloned.1.call-update) | async-done | bytes 131088 | tf_op jit(solution)/shard_map/psum | solution.py:109
  373.8 1.1 reduce_sum.55
  374.8 0.5 broadcast_multiply_fusion
  375.3 1.6 copy.71
  (29 shorter events, 0.2 us)
Async XLA Ops:
  7.2 111.4 %all-reduce.9.cloned.1.call-start = ((), (), s32[]{:S(2)}) async-start(), calls=%async_computation.6 | async-start | bytes 1048576 | tf_op jit(solution)/shard_map/psum | solution.py:9
  41.5 81.6 %all-to-all-start = ((bf16[8,2,4,32,2,128]{5,4,3,2,1,0:T(2,128)(2,1)}), bf16[8,2,4,32,2,128]{5,4,3,2,1,0:T(2,128)(2,1)S(1)}, u32[]{:S(2)}, u32[]{:S(2)}) async-start(bf16[8,2,4,32,2,128]{5,4,3,2,1,0:T(2,128)(2,1)} %param.4), calls=%async_computation | async-start | bytes 2097152 | tf_op jit(solution)/shard_map/all_to_all | solution.py:42
  45.8 165.8 %reduce-scatter.2.cloned.1.call-start = ((), (), s32[]{:S(2)}) async-start(), calls=%async_computation.3 | async-start | bytes 589824 | tf_op jit(solution)/shard_map/reduce_scatter | solution.py:71
  118.6 4.4 %copy-start.3 = (bf16[1,2,128,128]{3,2,0,1:T(8,128)(2,1)S(1)}, bf16[1,2,128,128]{3,2,0,1:T(8,128)(2,1)}, u32[]{:S(2)}) copy-start(bf16[1,2,128,128]{3,2,0,1:T(8,128)(2,1)} %get-tuple-element.18) | copy-start | bytes 196612
  118.6 4.4 %copy-start.2 = (bf16[1,2,128,128]{3,2,0,1:T(8,128)(2,1)S(1)}, bf16[1,2,128,128]{3,2,0,1:T(8,128)(2,1)}, u32[]{:S(2)}) copy-start(bf16[1,2,128,128]{3,2,0,1:T(8,128)(2,1)} %get-tuple-element.19) | copy-start | bytes 196612
  148.9 63.7 %copy-start.1 = (s32[8,4096]{1,0:T(8,128)S(1)}, s32[8,4096]{1,0:T(8,128)}, u32[]{:S(2)}) copy-start(s32[8,4096]{1,0:T(8,128)} %param.7) | copy-start | bytes 393220
  149.8 150.3 %all-reduce.5.cloned.1.call-start = ((), (), s32[]{:S(2)}) async-start(), calls=%async_computation.4 | async-start | bytes 262144 | tf_op jit(solution)/shard_map/psum | solution.py:109
  253.0 47.1 %copy-start = (bf16[4,32,2,128]{3,1,2,0:T(8,128)(2,1)S(1)}, bf16[4,32,2,128]{3,1,2,0:T(8,128)(2,1)}, u32[]{:S(2)}) copy-start(bf16[4,32,2,128]{3,1,2,0:T(8,128)(2,1)} %reduce-scatter.2.cloned.1.call-done) | copy-start | bytes 196612
  269.2 104.6 %all-reduce.7.cloned.1.call-start = ((), (), s32[]{:S(2)}) async-start(), calls=%async_computation.5 | async-start | bytes 262144 | tf_op jit(solution)/shard_map/psum | solution.py:109
Sparse Core Ops, SparseCore 0:
  41.6 76.9 all-reduce.8
  149.9 61.5 reduce-scatter.1
  269.3 30.7 all-reduce.4
  303.3 70.4 all-reduce.6
